TPU v7x, 16 devices: a 4x2x1 block of a 4x4x8 slice. The times are simulated.
16 devices in a mesh: dp: 2 (over y, z), tp: 8 (over x, core).
Axes of the slice: x: 4, y: 2, z: 1, core: 2. Of those that a mesh axis runs over, the one named last changes fastest.
The devices are a block of a 4x4x8 slice.
Arguments:
- x_a: bfloat16 [4096, 4608], P(('dp', 'tp')), parts along dimension 0
- x_b: bfloat16 [4096, 4608], P(('dp', 'tp')), parts along dimension 0
- labels_a: int32 [4096], P(('dp', 'tp')), parts along dimension 0
- labels_b: int32 [4096], P(('dp', 'tp')), parts along dimension 0
- w_head: bfloat16 [4608, 49152], P(None, 'tp')
Outputs:
- output 1: float32 [4], P('dp'), parts along dimension 0
- output 2: bfloat16 [9216, 49152], P('dp', 'tp'), parts along dimension 0
- output 3: bfloat16 [4096, 4608], P(('dp', 'tp')), parts along dimension 0
- output 4: bfloat16 [4096, 4608], P(('dp', 'tp')), parts along dimension 0
There are 2 independent parts. A program takes and returns all parts, laid end to end along the dimension named above; an argument that names none is the same for every part.
All inputs are finite; a program needn't handle non-finite values.
Results may differ from a plain program's by a relative error of at most 0.001.
Values are sent between devices in bfloat16 or wider.
A program may use at most 768 MiB of HBM per device.

v0:
```python
import jax
import jax.numpy as jnp
from jax import lax
from jax.sharding import PartitionSpec as P


def solution(mesh):
    group_size = mesh.shape["tp"]

    def local_step(x_a, x_b, labels_a, labels_b, w_local):
        tok_rows = x_a.shape[0]
        shard_cols = w_local.shape[1]
        tokens = tok_rows * group_size
        x_full = lax.all_gather(jnp.stack([x_a, x_b]), "tp", axis=1, tiled=True)
        label_full = lax.all_gather(jnp.stack([labels_a, labels_b]), "tp", axis=1, tiled=True)
        logits = jnp.einsum("mth,hv->mtv", x_full, w_local, preferred_element_type=jnp.float32)
        col_ids = lax.broadcasted_iota(jnp.int32, (1, 1, shard_cols), 2) + lax.axis_index("tp") * shard_cols
        label_hit = col_ids == label_full[..., None]
        local_target = jnp.sum(jnp.where(label_hit, logits, 0.0), axis=-1)
        row_max = lax.pmax(jnp.max(logits, axis=-1), "tp")
        shifted = jnp.exp(logits - row_max[..., None])
        stat_sums = lax.psum(jnp.stack([jnp.sum(shifted, axis=-1), local_target]), "tp")
        row_sum = stat_sums[0]
        loss_tok = row_max + jnp.log(row_sum) - stat_sums[1]
        losses = jnp.mean(loss_tok, axis=-1)
        grad_logits = ((shifted / row_sum[..., None] - label_hit.astype(jnp.float32)) / tokens).astype(jnp.bfloat16)
        grad_w = jnp.einsum("mth,mtv->hv", x_full, grad_logits, preferred_element_type=jnp.float32).astype(jnp.bfloat16)
        grad_part = jnp.einsum("mtv,hv->mth", grad_logits, w_local, preferred_element_type=jnp.float32)
        grad_x = lax.psum_scatter(grad_part, "tp", scatter_dimension=1, tiled=True).astype(jnp.bfloat16)
        return losses, grad_w, grad_x[0], grad_x[1]

    row_spec = P(("dp", "tp"), None)
    label_spec = P(("dp", "tp"))
    return jax.shard_map(local_step, mesh=mesh, in_specs=(row_spec, row_spec, label_spec, label_spec, P(None, "tp")), out_specs=(P("dp"), P("dp", "tp"), row_spec, row_spec), check_vma=False)
```

profile of v0, /device:TPU:112, one launch (start us, length us, event | category | flops | bytes accessed | tf_op | source)
XLA Modules:
  0.0 1188.0 jit_solution(6648007037495026144)
XLA Ops:
  7.2 0.1 all-gather.2.cloned.1.call-start
  7.2 5.0 pad_maximum_fusion
  12.3 0.1 reduce-scatter.2.cloned.1.call-start
  12.4 0.7 pad_add_fusion
  13.1 24.3 %all_gather.7 = s32[2,2048]{1,0:T(2,128)} all-gather(s32[2,256]{1,0:T(2,128)S(1)} %pad_add_fusion), channel_id=1, replica_groups=mesh['dp'=2,'tp'=8] {'tp'}, dimensions={1}, use_global_device_ids=true | all-gather | bytes 18432 | tf_op jit(solution)/shard_map/all_gather | solution.py:15
  37.4 0.6 iota_add_fusion
  38.0 146.8 %all-gather.2.cloned.1.call-done = bf16[2,2048,4608]{2,1,0:T(8,128)(2,1)} async-done(((bf16[2,256,4608]{2,1,0:T(8,128)(2,1)}), bf16[2,2048,4608]{2,1,0:T(8,128)(2,1)}) %all-gather.2.cloned.1.call-update) | async-done | bytes 37748752 | tf_op jit(solution)/shard_map/all_gather | solution.py:14
  184.8 248.0 %fusion.13 = (f32[2,2048]{1,0:T(2,128)S(1)}, f32[2,2048,6144]{2,1,0:T(8,128)}) fusion(bf16[2,2048,4608]{2,1,0:T(8,128)(2,1)} %all-gather.2.cloned.1.call-done, bf16[4608,6144]{1,0:T(8,128)(2,1)} %param.9), kind=kOutput, calls=%fused_computation.24 | convolution fusion | flops 231953399808 | bytes 195051520 | tf_op jit(solution)/shard_map/mth,hv->mtv/dot_general | solution.py:16
  432.7 24.1 %pmax.7 = f32[2,2048]{1,0:T(2,128)S(1)} all-reduce(f32[2,2048]{1,0:T(2,128)S(1)} %get-tuple-element.8), channel_id=1, replica_groups=mesh['dp'=2,'tp'=8] {'tp'}, use_global_device_ids=true, to_apply=%region_1.2 | all-reduce | flops 4096 | bytes 32768 | tf_op jit(solution)/shard_map/pmax | solution.py:20
  456.9 31.6 %fusion.4 = (f32[2,2048]{1,0:T(2,128)S(1)}, f32[2,2048]{1,0:T(2,128)S(1)}) fusion(f32[2,2048,6144]{2,1,0:T(8,128)} %get-tuple-element.9, f32[2,2048]{1,0:T(2,128)S(1)} %pmax.7, s32[2,2048]{1,0:T(2,128)S(1)} %copy-done.4, s32[6144]{0:T(1024)S(1)} %copy-done.2), kind=kLoop, calls=%fused_computation.8 | loop fusion | flops 125820928 | bytes 100753408 | tf_op jit(solution)/shard_map/reduce_sum | solution.py:22
  488.5 23.9 %psum.7 = f32[2,2,2048]{2,1,0:T(2,128)S(1)} all-reduce(f32[2,2,2048]{2,1,0:T(2,128)S(1)} %pad_maximum_fusion.1), channel_id=1, replica_groups=mesh['dp'=2,'tp'=8] {'tp'}, use_global_device_ids=true, to_apply=%region_4.5 | all-reduce | flops 8192 | bytes 65536 | tf_op jit(solution)/shard_map/psum | solution.py:22
  512.4 0.6 copy-done.8
  513.0 49.2 %fusion.24 = bf16[2,2048,6144]{2,1,0:T(8,128)(2,1)} fusion(f32[2,2048,6144]{2,1,0:T(8,128)} %get-tuple-element.9, f32[2,2048]{1,0:T(2,128)S(1)} %slice_bitcast_fusion.3, s32[2,2048]{1,0:T(2,128)S(1)} %copy-done.4, s32[6144]{0:T(1024)S(1)} %copy-done.2, f32[2,2048]{1,0:T(2,128)S(1)} %pmax.7), kind=kLoop, calls=%fused_computation.6.clone.clone.1 | loop fusion | flops 176160768 | bytes 151068672 | tf_op jit(solution)/shard_map/mtv,hv->mth/dot_general | solution.py:28
  562.2 249.9 %fusion.5 = f32[2,2048,4608]{2,1,0:T(8,128)} fusion(bf16[4608,6144]{1,0:T(8,128)(2,1)} %param.9, bf16[2,2048,6144]{2,1,0:T(8,128)(2,1)} %fusion.24), kind=kOutput, calls=%fused_computation.9 | convolution fusion | flops 231928233984 | bytes 182452224 | tf_op jit(solution)/shard_map/mtv,hv->mth/dot_general | solution.py:28
  812.2 0.1 reduce-scatter.2.cloned.1.call-update
  812.2 0.6 copy-done.1
  812.8 0.1 copy-done.7
  812.9 0.1 fusion.10
  813.0 0.5 broadcast_multiply_fusion
  813.6 49.2 %fusion.22 = bf16[2,2048,6144]{2,1,0:T(8,128)(2,1)} fusion(f32[2,2048,6144]{2,1,0:T(8,128)} %get-tuple-element.9, f32[2,2048]{1,0:T(2,128)S(1)} %copy-done.9, s32[2,2048]{1,0:T(2,128)S(1)} %copy-done.5, s32[6144]{0:T(1024)S(1)} %copy-done.3, f32[2,2048]{1,0:T(2,128)S(1)} %copy-done.1), kind=kLoop, calls=%fused_computation.6.clone.1.clone.1 | loop fusion | flops 176160768 | bytes 151068672 | tf_op jit(solution)/shard_map/mth,mtv->hv/dot_general | solution.py:27
  862.8 248.5 %bitcast_convert_fusion = bf16[4608,6144]{1,0:T(8,128)(2,1)} fusion(bf16[2,2048,4608]{2,1,0:T(8,128)(2,1)} %all-gather.2.cloned.1.call-done, bf16[2,2048,6144]{2,1,0:T(8,128)(2,1)} %fusion.22), kind=kOutput, calls=%fused_computation.2 | convolution fusion | flops 231956545536 | bytes 144703488 | tf_op jit(solution)/shard_map/mth,mtv->hv/dot_general | solution.py:27
  1111.3 63.2 %reduce-scatter.2.cloned.1.call-done = f32[2,256,4608]{2,1,0:T(8,128)} async-done(((f32[2,2048,4608]{2,1,0:T(8,128)}), f32[2,256,4608]{2,1,0:T(8,128)}) %reduce-scatter.2.cloned.1.call-update) | async-done | bytes 9437200 | tf_op jit(solution)/shard_map/reduce_scatter | solution.py:29
  1174.4 4.2 convert_element_type.15
  1178.6 2.5 slice_bitcast_fusion
  (20 shorter events, 0.1 us)
Async XLA Ops:
  7.2 177.6 %all-gather.2.cloned.1.call-start = ((), (), s32[]{:S(2)}) async-start(), calls=%async_computation.1 | async-start | bytes 42467328 | tf_op jit(solution)/shard_map/all_gather | solution.py:14
  12.3 1162.1 %reduce-scatter.2.cloned.1.call-start = ((), (), s32[]{:S(2)}) async-start(), calls=%async_computation.2 | async-start | bytes 84934656 | tf_op jit(solution)/shard_map/reduce_scatter | solution.py:29
  184.8 272.1 %copy-start.2 = (s32[6144]{0:T(1024)S(1)}, s32[6144]{0:T(1024)}, u32[]{:S(2)}) copy-start(s32[6144]{0:T(1024)} %iota_add_fusion) | copy-start | bytes 73732
  184.8 272.1 %copy-start.4 = (s32[2,2048]{1,0:T(2,128)S(1)}, s32[2,2048]{1,0:T(2,128)}, u32[]{:S(2)}) copy-start(s32[2,2048]{1,0:T(2,128)} %all_gather.7) | copy-start | bytes 49156
  456.9 105.3 %copy-start = (f32[2,2048]{1,0:T(2,128)}, f32[2,2048]{1,0:T(2,128)S(1)}, u32[]{:S(2)}) copy-start(f32[2,2048]{1,0:T(2,128)S(1)} %pmax.7) | copy-start | bytes 49156
  512.3 49.8 %copy-start.6 = (f32[2,2,2048]{2,1,0:T(2,128)}, f32[2,2,2048]{2,1,0:T(2,128)S(1)}, u32[]{:S(2)}) copy-start(f32[2,2,2048]{2,1,0:T(2,128)S(1)} %psum.7) | copy-start | bytes 98308
  512.4 0.6 copy-start.8
  812.1 0.7 copy-start.1
  812.1 0.8 copy-start.7
  812.1 1.4 copy-start.3
  812.1 1.4 copy-start.5
  812.1 1.4 copy-start.9
Sparse Core Ops, SparseCore 0:
  12.4 172.2 all-gather.1
  812.3 362.0 reduce-scatter.1
where the time goes:
time: 1190 us
  matrix products  746 us (63%)
  waiting for transfers between devices  210 us (18%)
  other arithmetic  141 us (12%)
  blocking collectives  72.3 us (6%)
  between operations  14.1 us (1%)
    dot_general x1, matrix products, local_step(): jnp.einsum('mtv,hv->mth', grad_logits, w_local, preferred_element_type=jn...  250 us
    dot_general x1, matrix products, local_step(): jnp.einsum('mth,mtv->hv', x_full, grad_logits, preferred_element_type=jnp...  248 us
    dot_general x1, matrix products, local_step(): jnp.einsum('mth,hv->mtv', x_full, w_local, preferred_element_type=jnp.flo...  248 us
    all_gather x1, waiting for transfers between devices, local_step(): x_full = lax.all_gather(jnp.stack([x_a, x_b]), 'tp', axis=1, tiled=True)  147 us
    reduce_scatter x1, waiting for transfers between devices, local_step(): lax.psum_scatter(grad_part, 'tp', scatter_dimension=1, tiled=True)  63.2 us
    dot_general x1, other arithmetic, local_step(): jnp.einsum('mth,mtv->hv', x_full, grad_logits, preferred_element_type=jnp...  49.2 us
    dot_general x1, other arithmetic, local_step(): jnp.einsum('mtv,hv->mth', grad_logits, w_local, preferred_element_type=jn...  49.2 us
    reduce_sum x1, other arithmetic, local_step(): jnp.sum(shifted, axis=-1)  31.6 us
  transfers between devices with their start and end apart: 2, of which 2 were waited for; matrix products, arithmetic and copies ran while one was open for 25% of the time, Pallas kernels for 0%

commit v1 on v0

v1 whole, which is shorter than its diff:
```python
import functools

import jax
import jax.numpy as jnp
from jax import lax
from jax.experimental import pallas as pl
from jax.experimental.pallas import tpu as pltpu
from jax.sharding import PartitionSpec as P

F32 = jnp.float32
BF16 = jnp.bfloat16
LOWEST = -3.4028235e38
VMEM_BYTES = 67043328
LANES = 128
CHIPS = 4
PHASES = 2 * CHIPS
LOGIT_COLS, LOGIT_SUB = 1024, 512
G_ROWS, G_COLS, X_TILE, X_SUB, PART = 1024, 768, 512, 512, 32
PARTNER, RIGHT, LEFT, FORWARD_RIGHT, FORWARD_LEFT, PASS_RIGHT, PASS_LEFT, PASS_FIRST, PASS_SECOND = range(9)


def phase_block(phase, chip):
    turn = lax.rem(phase + 1, 3)
    away = lax.min(lax.div(phase, 2), 1) * (1 + 2 * turn - 3 * lax.div(turn, 2))
    batch = lax.div(phase, 5) + 1 - lax.min((phase - 1) * (phase - 1), 1)
    return batch, lax.rem(chip + away, CHIPS)


def logits_kernel(
    x_a, x_b, lab, w_ref, z_ref, x_full, lab_full, stat_full,
    x_buf, run_max, run_sum, stat,
    send_sem, recv_sem, lab_send, lab_recv, stat_send, stat_recv, own_sem, keep_sem, load_sem,
    *, group, sub,
):
    phase, step = pl.program_id(0), pl.program_id(1)
    steps = pl.num_programs(1)
    rows, cols = z_ref.shape
    unit = x_a.shape[0]
    half = unit // 2
    tokens = unit * group
    me = lax.axis_index("tp")
    chip, core = lax.div(me, 2), lax.rem(me, 2)
    partner = chip * 2 + 1 - core
    device = lambda hops: lax.rem(chip + hops, CHIPS) * 2 + core
    right, opposite, left = device(1), device(2), device(3)
    x_own = (x_a, x_b)

    def rows_of(batch, dev, first=0, size=unit):
        return x_full.at[pl.ds(pl.multiple_of(batch * tokens + dev * unit + first, half), size)]

    def copy(kind, batch):
        src = dst = None
        if kind == PARTNER:
            src, to = x_own[batch], partner
            dst = x_buf.at[batch, pl.ds(pl.multiple_of(core * unit, half), unit)]
        elif kind in (RIGHT, LEFT):
            src, to = x_own[batch], right if kind == RIGHT else left
            dst = rows_of(batch, me)
        elif kind == FORWARD_RIGHT:
            src, to = rows_of(batch, left, 0, half), right
        elif kind == FORWARD_LEFT:
            src, to = rows_of(batch, right, half, half), left
        elif kind == PASS_RIGHT:
            src, to = rows_of(batch, right), partner
        elif kind == PASS_LEFT:
            src, to = rows_of(batch, left), partner
        elif kind == PASS_FIRST:
            src, to = rows_of(batch, opposite, 0, half), partner
        else:
            src, to = rows_of(batch, opposite, half, half), partner
        return pltpu.make_async_remote_copy(
            src_ref=src, dst_ref=src if dst is None else dst,
            send_sem=send_sem.at[kind, batch], recv_sem=recv_sem.at[kind, batch],
            device_id={"tp": to}, device_id_type=pl.DeviceIdType.MESH,
        )

    def label_copy(k):
        return pltpu.make_async_remote_copy(
            src_ref=lab, dst_ref=lab_full.at[me], send_sem=lab_send.at[k], recv_sem=lab_recv.at[k],
            device_id={"tp": lax.rem(me + k, group)}, device_id_type=pl.DeviceIdType.MESH,
        )

    def stat_copy(batch, k):
        return pltpu.make_async_remote_copy(
            src_ref=stat.at[batch], dst_ref=stat_full.at[me, batch],
            send_sem=stat_send.at[batch, k], recv_sem=stat_recv.at[batch, k],
            device_id={"tp": lax.rem(me + k, group)}, device_id_type=pl.DeviceIdType.MESH,
        )

    def own_load(batch):
        return pltpu.make_async_copy(
            x_own[batch], x_buf.at[batch, pl.ds(pl.multiple_of(core * unit, half), unit)], own_sem.at[batch]
        )

    def own_keep(batch):
        return pltpu.make_async_copy(x_buf.at[batch], rows_of(batch, chip * 2, 0, 2 * unit), keep_sem.at[batch])

    def load(to_phase):
        batch, away = phase_block(jnp.int32(to_phase), chip)
        return pltpu.make_async_copy(rows_of(batch, away * 2, 0, 2 * unit), x_buf.at[to_phase % 2], load_sem)

    label_own = pltpu.make_async_copy(lab, lab_full.at[me], own_sem.at[2])
    stat_own = lambda batch: pltpu.make_async_copy(stat.at[batch], stat_full.at[me, batch], own_sem.at[3 + batch])
    at = lambda p, s: pl.when((phase == p) & (step == s))
    last = steps - 1
    others = range(1, group)

    @at(0, 0)
    def _():
        barrier = pltpu.get_barrier_semaphore()
        for k in others:
            pl.semaphore_signal(
                barrier, inc=1, device_id={"tp": lax.rem(me + k, group)}, device_id_type=pl.DeviceIdType.MESH
            )
        own_load(0).start()
        own_load(1).start()
        pl.semaphore_wait(barrier, group - 1)
        copy(PARTNER, 0).start()
        copy(RIGHT, 0).start()
        copy(LEFT, 0).start()
        copy(PARTNER, 1).start()
        for k in others:
            label_copy(k).start()
        label_own.start()
        own_load(0).wait()
        copy(PARTNER, 0).wait_recv()
        own_keep(0).start()

    @at(0, last)
    def _():
        own_load(1).wait()
        copy(PARTNER, 1).wait_recv()
        own_keep(1).start()

    def arrived(batch):
        copy(RIGHT, batch).wait_recv()
        copy(LEFT, batch).wait_recv()
        copy(FORWARD_RIGHT, batch).start()
        copy(FORWARD_LEFT, batch).start()
        copy(PASS_RIGHT, batch).start()
        copy(PASS_LEFT, batch).start()

    def arrived_far(batch):
        copy(FORWARD_RIGHT, batch).wait_recv()
        copy(FORWARD_LEFT, batch).wait_recv()
        copy(PASS_FIRST, batch).start()
        copy(PASS_SECOND, batch).start()

    @at(1, (7 * steps) // 12)
    def _():
        arrived(0)
        copy(RIGHT, 1).start()
        copy(LEFT, 1).start()

    @at(1, last)
    def _():
        own_keep(0).wait()
        copy(PASS_RIGHT, 0).wait_recv()
        load(2).start()

    @at(2, (8 * steps) // 12)
    def _():
        arrived_far(0)

    @at(2, last)
    def _():
        own_keep(1).wait()
        copy(PASS_LEFT, 0).wait_recv()
        load(3).start()

    @at(3, last)
    def _():
        copy(PASS_FIRST, 0).wait_recv()
        copy(PASS_SECOND, 0).wait_recv()
        load(4).start()

    @at(4, (4 * steps) // 12)
    def _():
        arrived(1)

    @at(4, last)
    def _():
        copy(PASS_RIGHT, 1).wait_recv()
        load(5).start()

    @at(5, 1)
    def _():
        for k in others:
            stat_copy(0, k).start()
        stat_own(0).start()

    @at(5, (6 * steps) // 12)
    def _():
        arrived_far(1)

    @at(5, last)
    def _():
        copy(PASS_LEFT, 1).wait_recv()
        load(6).start()

    @at(6, last)
    def _():
        copy(PASS_FIRST, 1).wait_recv()
        copy(PASS_SECOND, 1).wait_recv()
        load(7).start()

    @pl.when((step == 0) & (phase >= 2))
    def _():
        load(2).wait()

    @pl.when(step == 0)
    def _():
        run_max[...] = jnp.full_like(run_max, LOWEST)
        run_sum[...] = jnp.zeros_like(run_sum)

    x = x_buf.at[lax.rem(phase, 2)]
    for r in range(0, rows, sub):
        tile = jnp.dot(x[r : r + sub, :], w_ref[...], preferred_element_type=F32)
        z_ref[r : r + sub, :] = tile
        old = run_max[r : r + sub, :]
        new = old
        for c in range(0, cols, LANES):
            new = jnp.maximum(new, tile[:, c : c + LANES])
        total = run_sum[r : r + sub, :] * jnp.exp(old - new)
        for c in range(0, cols, LANES):
            total = total + jnp.exp(tile[:, c : c + LANES] - new)
        run_max[r : r + sub, :] = new
        run_sum[r : r + sub, :] = total

    @pl.when(step == last)
    def _():
        batch, away = phase_block(phase, chip)
        spot = pl.ds(pl.multiple_of(away * rows, rows), rows)
        lane_max = run_max[...].T
        top = jnp.max(lane_max, axis=0, keepdims=True)
        stat[batch, 0:1, spot] = top
        stat[batch, 1:2, spot] = jnp.sum(run_sum[...].T * jnp.exp(lane_max - top), axis=0, keepdims=True)

    @at(PHASES - 1, last)
    def _():
        for kind in range(9):
            for batch in range(2):
                copy(kind, batch).wait_send()
        for k in others:
            label_copy(k).wait()
        label_own.wait()
        for k in others:
            stat_copy(1, k).start()
        stat_own(1).start()
        for batch in range(2):
            for k in others:
                stat_copy(batch, k).wait()
            stat_own(batch).wait()


def gather_logits(x_a, x_b, lab, w, group):
    unit, hidden = x_a.shape
    vocab = w.shape[1]
    tokens = unit * group
    rows, cols, sub = 2 * unit, LOGIT_COLS, LOGIT_SUB

    def z_block(phase, step):
        batch, away = phase_block(phase, lax.div(lax.axis_index("tp"), 2))
        return batch * CHIPS + away, step

    hbm = pl.BlockSpec(memory_space=pl.ANY)
    dma = pltpu.SemaphoreType.DMA
    return pl.pallas_call(
        functools.partial(logits_kernel, group=group, sub=sub),
        grid=(PHASES, vocab // cols),
        in_specs=[hbm, hbm, hbm, pl.BlockSpec((hidden, cols), lambda p, n: (0, n))],
        out_specs=[pl.BlockSpec((rows, cols), z_block), hbm, hbm, hbm],
        out_shape=[
            jax.ShapeDtypeStruct((2 * tokens, vocab), F32),
            jax.ShapeDtypeStruct((2 * tokens, hidden), BF16),
            jax.ShapeDtypeStruct((group, 2, unit), jnp.int32),
            jax.ShapeDtypeStruct((group, 2, 2, tokens), F32),
        ],
        scratch_shapes=[
            pltpu.VMEM((2, rows, hidden), BF16),
            pltpu.VMEM((rows, LANES), F32),
            pltpu.VMEM((rows, LANES), F32),
            pltpu.VMEM((2, 2, tokens), F32),
            dma((9, 2)), dma((9, 2)), dma((group,)), dma((group,)), dma((2, group)), dma((2, group)),
            dma((5,)), dma((2,)), dma,
        ],
        compiler_params=pltpu.CompilerParams(
            vmem_limit_bytes=VMEM_BYTES, collective_id=0, has_side_effects=True,
            dimension_semantics=("arbitrary", "arbitrary"),
        ),
        cost_estimate=pl.CostEstimate(
            flops=4 * tokens * hidden * vocab, bytes_accessed=8 * tokens * vocab, transcendentals=0
        ),
        name="gather_logits",
    )(x_a, x_b, lab, w)


def grad_x_kernel(*refs, first, blocks, inv_tokens, resume):
    if resume:
        z_ref, w_ref, top_ref, inv_ref, lab_ref, g_in, g_ref, dx_ref, hit_ref, g_even, g_odd, hits, sem = refs
    else:
        z_ref, w_ref, top_ref, inv_ref, lab_ref, g_ref, dx_ref, hit_ref, g_even, g_odd, hits = refs
    block, step = pl.program_id(0), pl.program_id(1)
    steps = pl.num_programs(1)
    rows, cols = z_ref.shape
    chunks = g_even.shape[1] // cols

    def make_g(dst):
        begin = jnp.minimum(step, chunks - 1) * cols
        lane = lax.broadcasted_iota(jnp.int32, (1, LANES), 1) + begin
        for r in range(0, rows, PART):
            here = slice(r, r + PART)
            top, inv, lab, found = top_ref[here, :], inv_ref[here, :], lab_ref[here, :], hits[here, :]
            for c in range(0, cols, LANES):
                z = z_ref[here, c : c + LANES]
                hit = lane + c == lab
                found = jnp.where(hit, z, found)
                g = (jnp.exp(z - top) * inv - jnp.where(hit, inv_tokens, 0.0)).astype(BF16)
                g_ref[here, c : c + LANES] = g
                if dst is not None:
                    dst[here, pl.ds(pl.multiple_of(begin + c, LANES), LANES)] = g
            hits[here, :] = found

    def product(src):
        for r in range(0, rows, X_SUB):
            dx_ref[r : r + X_SUB, :] = lax.dot_general(
                src[r : r + X_SUB, :], w_ref[...], (((1,), (1,)), ((), ())), preferred_element_type=F32
            )

    @pl.when(step == 0)
    def _():
        hits[...] = jnp.zeros_like(hits)

    if resume:
        @pl.when((block == 0) & (step == 0))
        def _():
            fetch = pltpu.make_async_copy(g_in.at[pl.ds(first * rows, rows)], g_even, sem)
            fetch.start()
            fetch.wait()

        @pl.when(block == 0)
        def _():
            product(g_even)
            make_g(g_odd)

        @pl.when(block == 1)
        def _():
            product(g_odd)
    else:
        @pl.when((block == 0) & (step < chunks))
        def _():
            make_g(g_even)

        @pl.when(block == 1)
        def _():
            product(g_even)
            make_g(g_odd)

        @pl.when(block == 2)
        def _():
            product(g_odd)
            make_g(None)

    @pl.when(step == steps - 1)
    def _():
        hit_ref[...] = jnp.sum(hits[...].reshape(-1, 8, LANES), axis=0)


def grad_x_call(z, w, top, inv, lab, inv_tokens, g=None):
    total, vocab = z.shape
    hidden = w.shape[0]
    blocks = total // G_ROWS // 2
    assert blocks == 2
    resume = g is not None
    steps, chunks = hidden // X_TILE, vocab // G_COLS
    bound = lambda h: jnp.minimum(h, chunks - 1)
    if resume:
        grid = (blocks, steps)
        row = lambda i: 2 * blocks - 1
        chunk = lambda i, h: (row(i), jnp.where(i == 0, bound(h), chunks - 1))
        w_block = lambda i, h: (h, 0)
        dx_block = lambda i, h: (i, h)
    else:
        grid = (blocks + 1, steps)
        row = lambda i: i
        chunk = lambda i, h: (i, bound(h))
        w_block = lambda i, h: (jnp.where(i == 0, 0, h), 0)
        dx_block = lambda i, h: (jnp.maximum(i - 1, 0), jnp.where(i == 0, 0, h))
    stat = pl.BlockSpec((G_ROWS, LANES), lambda i, h: (row(i), 0))
    scratch = [pltpu.VMEM((G_ROWS, vocab), BF16)] * 2 + [pltpu.VMEM((G_ROWS, LANES), F32)]
    return pl.pallas_call(
        functools.partial(grad_x_kernel, first=blocks, blocks=blocks, inv_tokens=inv_tokens, resume=resume),
        grid=grid,
        in_specs=[pl.BlockSpec((G_ROWS, G_COLS), chunk), pl.BlockSpec((X_TILE, vocab), w_block), stat, stat, stat]
        + ([pl.BlockSpec(memory_space=pl.ANY)] if resume else []),
        out_specs=[
            pl.BlockSpec((G_ROWS, G_COLS), chunk),
            pl.BlockSpec((G_ROWS, X_TILE), dx_block),
            pl.BlockSpec((8, LANES), lambda i, h: (i, 0)),
        ],
        out_shape=[
            jax.ShapeDtypeStruct((total, vocab), BF16),
            jax.ShapeDtypeStruct((total // 2, hidden), F32),
            jax.ShapeDtypeStruct((8 * grid[0], LANES), F32),
        ],
        scratch_shapes=scratch + ([pltpu.SemaphoreType.DMA] if resume else []),
        input_output_aliases={5: 0} if resume else {},
        compiler_params=pltpu.CompilerParams(vmem_limit_bytes=VMEM_BYTES),
        cost_estimate=pl.CostEstimate(flops=total * hidden * vocab, bytes_accessed=3 * total * vocab, transcendentals=0),
        name="grad_x_b" if resume else "grad_x_a",
    )(z, w, top, inv, lab, *([g] if resume else []))


def solution(mesh):
    group = mesh.shape["tp"]

    def local_step(x_a, x_b, labels_a, labels_b, w):
        vocab = w.shape[1]
        tokens = x_a.shape[0] * group
        z, x_full, labels, stats = gather_logits(x_a, x_b, jnp.stack([labels_a, labels_b]), w, group)
        row_max = jnp.max(stats[:, :, 0], axis=0)
        row_sum = jnp.sum(stats[:, :, 1] * jnp.exp(stats[:, :, 0] - row_max), axis=0)
        labels = jnp.transpose(labels, (1, 0, 2)).reshape(-1) - lax.axis_index("tp") * vocab
        spread = lambda a: jnp.broadcast_to(a.reshape(-1, 1), (2 * tokens, LANES))
        top, inv, lab = spread(row_max), spread(1.0 / (row_sum * tokens)), spread(labels)
        g, part_a, hit_a = grad_x_call(z, w, top, inv, lab, 1.0 / tokens)
        grad_x_a = lax.psum_scatter(part_a, "tp", scatter_dimension=0, tiled=True).astype(BF16)
        g, part_b, hit_b = grad_x_call(z, w, top, inv, lab, 1.0 / tokens, g)
        grad_x_b = lax.psum_scatter(part_b, "tp", scatter_dimension=0, tiled=True).astype(BF16)
        own = jnp.stack([jnp.sum(hit_a[:16]), jnp.sum(hit_a[16:]) + jnp.sum(hit_b[:8])])
        target = lax.psum(own, "tp")
        losses = jnp.mean(row_max + jnp.log(row_sum), axis=-1) - target / tokens
        pair = lambda a: a.reshape(2, tokens, -1)
        grad_w = jnp.einsum("mth,mtv->hv", pair(x_full), pair(g), preferred_element_type=F32).astype(BF16)
        return losses, grad_w, grad_x_a, grad_x_b

    rows, labs = P(("dp", "tp"), None), P(("dp", "tp"))
    return jax.shard_map(
        local_step,
        mesh=mesh,
        in_specs=(rows, rows, labs, labs, P(None, "tp")),
        out_specs=(P("dp"), P("dp", "tp"), rows, rows),
        check_vma=False,
    )
```

time: 1190 us -> 1000 us (0.84)
  Pallas kernels: 0 us -> 588 us
  matrix products: 746 us -> 248 us
  other arithmetic: 141 us -> 13.8 us
  waiting for transfers between devices: 210 us -> 105 us
  blocking collectives: 72.3 us -> 14.4 us
    pallas_call x0 -> x3, Pallas kernels: none -> 588 us  [the longest x2 306 us: grad_x_call(): pl.pallas_call(functools.partial(grad_x_kernel, first=blocks, blocks=bloc...]
    dot_general x3 -> x1, matrix products: 746 us -> 248 us  [local_step(): jnp.einsum('mth,mtv->hv', pair(x_full), pair(g), preferred_element_type=F32)]
    all_gather x1 -> x0, waiting for transfers between devices: 147 us -> none  [local_step(): x_full = lax.all_gather(jnp.stack([x_a, x_b]), 'tp', axis=1, tiled=True)]
    dot_general x2 -> x0, other arithmetic: 98.5 us -> none  [the longest x1 49.2 us: local_step(): jnp.einsum('mth,mtv->hv', x_full, grad_logits, preferred_element_type=jnp...]
    reduce_scatter x1 -> x2, waiting for transfers between devices: 63.2 us -> 104 us  [the longest x1 104 us: local_step(): lax.psum_scatter(part_a, 'tp', scatter_dimension=0, tiled=True).astype(BF16)]
    reduce_sum x2 -> x5, other arithmetic: 31.7 us -> 2.56 us  [the longest x1 0.65 us: local_step(): losses = jnp.mean(row_max + jnp.log(row_sum), axis=-1) - target / tokens]
    all_gather x1 -> x0, blocking collectives: 24.3 us -> none  [local_step(): lax.all_gather(jnp.stack([labels_a, labels_b]), 'tp', axis=1, tiled=True)]
    pmax x1 -> x0, blocking collectives: 24.1 us -> none  [local_step(): row_max = lax.pmax(jnp.max(logits, axis=-1), 'tp')]
  transfers between devices with their start and end apart: 2 -> 2, of which waited for: 2 -> 1; matrix products, arithmetic and copies ran while one was open for 25% -> 26% of each run, Pallas kernels for 0% -> 0%
where the time goes in v1:
time: 1000 us; the launch traced here: 994 us
  Pallas kernels  588 us (59%)
  matrix products  248 us (25%)
  waiting for transfers between devices  105 us (10%)
  between operations  15.7 us (2%)
  blocking collectives  14.4 us (1%)
  other arithmetic  13.8 us (1%)
    pallas_call x2, Pallas kernels, grad_x_call(): pl.pallas_call(functools.partial(grad_x_kernel, first=blocks, blocks=bloc...  306 us
    pallas_call x1, Pallas kernels, gather_logits(): pl.pallas_call(functools.partial(logits_kernel, group=group, sub=sub), gr...  282 us
    dot_general x1, matrix products, local_step(): jnp.einsum('mth,mtv->hv', pair(x_full), pair(g), preferred_element_type=F32)  248 us
    reduce_scatter x1, waiting for transfers between devices, local_step(): lax.psum_scatter(part_a, 'tp', scatter_dimension=0, tiled=True).astype(BF16)  104 us
  transfers between devices with their start and end apart: 2, of which 1 were waited for; matrix products, arithmetic and copies ran while one was open for 26% of the time, Pallas kernels for 0%

profile of v1, /device:TPU:112, one launch (start us, length us, event | category | flops | bytes accessed | tf_op | source)
XLA Modules:
  0.0 994.2 jit_solution(7195288797548069932)
XLA Ops:
  7.3 1.3 pad_add_fusion.lab
  8.5 281.9 %gather_logits.1 = (f32[4096,6144]{1,0:T(8,128)}, bf16[4096,4608]{1,0:T(8,128)(2,1)}, s32[8,2,256]{2,1,0:T(2,128)}, f32[8,2,2,2048]{3,2,1,0:T(2,128)}) custom-call(bf16[256,4608]{1,0:T(8,128)(2,1)} %x_a.1, bf16[256,4608]{1,0:T(8,128)(2,1)} %x_b.1, s32[2,256]{1,0:T(2,128)} %pad_add_fusion.lab, bf16[4608,6144]{1,0:T(8,128)(2,1)} %refs_1_.3), custom_call_target="tpu_custom_call" | custom-call | flops 231928233984 | bytes 100663296 | tf_op jit(solution)/shard_map/gather_logits/pallas_call | solution.py:268
  290.5 1.1 slice.17
  291.6 1.2 copy.11
  292.7 0.7 subtract_bitcast_fusion
  293.5 0.1 fusion
  293.7 0.6 add_reduce_fusion
  294.3 1.9 broadcast_in_dim.9.refs_2_
  296.2 1.9 broadcast_in_dim.20.refs_3_
  298.2 2.9 broadcast_in_dim.21.refs_4_
  301.0 163.4 %grad_x_a.1 = (bf16[4096,6144]{1,0:T(8,128)(2,1)}, f32[2048,4608]{1,0:T(8,128)}, f32[24,128]{1,0:T(8,128)}) custom-call(f32[4096,6144]{1,0:T(8,128)} %get-tuple-element.15.refs_0_, bf16[4608,6144]{1,0:T(8,128)(2,1)} %refs_1_.3, f32[4096,128]{1,0:T(8,128)} %broadcast_in_dim.9.refs_2_, f32[4096,128]{1,0:T(8,128)} %broadcast_in_dim.20.refs_3_, ...), custom_call_target="tpu_custom_call" | custom-call | flops 115964116992 | bytes 75497472 | tf_op jit(solution)/shard_map/grad_x_a/pallas_call | solution.py:391
  464.5 142.9 %grad_x_b.1 = (bf16[4096,6144]{1,0:T(8,128)(2,1)}, f32[2048,4608]{1,0:T(8,128)}, f32[16,128]{1,0:T(8,128)}) custom-call(f32[4096,6144]{1,0:T(8,128)} %get-tuple-element.15.refs_0_, bf16[4608,6144]{1,0:T(8,128)(2,1)} %refs_1_.3, f32[4096,128]{1,0:T(8,128)} %broadcast_in_dim.9.refs_2_, ...), custom_call_target="tpu_custom_call", output_to_operand_aliasing={{0}: (5, {})} | custom-call | flops 115964116992 | bytes 75497472 | tf_op jit(solution)/shard_map/grad_x_b/pallas_call | solution.py:391
  607.5 0.1 reduce-scatter.3.cloned.1.call-start
  607.6 0.7 reduce-scatter.3.cloned.1.call-update
  608.3 0.6 slice_reduce_fusion.3
  608.9 0.6 slice_reduce_fusion.2
  610.8 0.6 slice_reduce_fusion.1
  611.4 0.7 pad_maximum_fusion
  612.1 14.4 %psum.7 = f32[2]{0:T(128)S(1)} all-reduce(f32[2]{0:T(128)S(1)} %pad_maximum_fusion), channel_id=1, replica_groups=mesh['dp'=2,'tp'=8] {'tp'}, use_global_device_ids=true, to_apply=%region_6.0 | all-reduce | flops 2 | bytes 16 | tf_op jit(solution)/shard_map/psum | solution.py:431
  626.5 0.5 multiply_subtract_fusion
  627.0 248.5 %convolution_convert_fusion = bf16[4608,6144]{1,0:T(8,128)(2,1)} fusion(bf16[4096,4608]{1,0:T(8,128)(2,1)} %get-tuple-element.20, bf16[4096,6144]{1,0:T(8,128)(2,1)} %get-tuple-element.21), kind=kOutput, calls=%fused_computation | convolution fusion | flops 231956545536 | bytes 144703488 | tf_op jit(solution)/shard_map/mth,mtv->hv/dot_general | solution.py:434
  875.5 4.0 convert_element_type.11
  879.4 103.8 %reduce-scatter.3.cloned.1.call-done = f32[256,4608]{1,0:T(8,128)} async-done(((f32[2048,4608]{1,0:T(8,128)}), f32[256,4608]{1,0:T(8,128)}) %reduce-scatter.3.cloned.1.call-update) | async-done | bytes 4718608 | tf_op jit(solution)/shard_map/reduce_scatter | solution.py:427
  983.2 4.0 convert_element_type.10
  (14 shorter events, 0.2 us)
Async XLA Ops:
  7.2 868.3 %reduce-scatter.5.cloned.1.call-start = ((), (), s32[]{:S(2)}) async-start(), calls=%async_computation.3 | async-start | bytes 42467328 | tf_op jit(solution)/shard_map/reduce_scatter | solution.py:429
  607.4 0.9 copy-start
  607.4 1.5 copy-start.1
  607.4 19.1 %copy-start.2 = (f32[2]{0:T(128)S(1)}, f32[2]{0:T(128)}, u32[]{:S(2)}) copy-start(f32[2]{0:T(128)} %get-tuple-element.24) | copy-start | bytes 28
  607.5 375.7 %reduce-scatter.3.cloned.1.call-start = ((), (), s32[]{:S(2)}) async-start(), calls=%async_computation.2 | async-start | bytes 42467328 | tf_op jit(solution)/shard_map/reduce_scatter | solution.py:427
Sparse Core Ops, SparseCore 0:
  607.6 187.4 reduce-scatter.4
  797.4 185.7 reduce-scatter.2

commit v2 on v1

--- a/solution.py
+++ b/solution.py
@@ -6,6 +6,7 @@
 from jax.experimental import pallas as pl
 from jax.experimental.pallas import tpu as pltpu
 from jax.sharding import PartitionSpec as P
+
 
 F32 = jnp.float32
 BF16 = jnp.bfloat16
@@ -15,7 +16,7 @@
 CHIPS = 4
 PHASES = 2 * CHIPS
 LOGIT_COLS, LOGIT_SUB = 1024, 512
-G_ROWS, G_COLS, X_TILE, X_SUB, PART = 1024, 768, 512, 512, 32
+G_ROWS, G_COLS, X_TILE, X_SUB, PART, MIX = 1024, 768, 512, 256, 8, 256
 PARTNER, RIGHT, LEFT, FORWARD_RIGHT, FORWARD_LEFT, PASS_RIGHT, PASS_LEFT, PASS_FIRST, PASS_SECOND = range(9)
 
 
@@ -295,7 +296,46 @@
     )(x_a, x_b, lab, w)
 
 
-def grad_x_kernel(*refs, first, blocks, inv_tokens, resume):
+def share_kernel(own, all_ref, send_sem, recv_sem, keep_sem, *, group):
+    me = lax.axis_index("tp")
+    others = range(1, group)
+
+    def copy(k):
+        return pltpu.make_async_remote_copy(
+            src_ref=own, dst_ref=all_ref.at[me], send_sem=send_sem.at[k], recv_sem=recv_sem.at[k],
+            device_id={"tp": lax.rem(me + k, group)}, device_id_type=pl.DeviceIdType.MESH,
+        )
+
+    barrier = pltpu.get_barrier_semaphore()
+    for k in others:
+        pl.semaphore_signal(
+            barrier, inc=1, device_id={"tp": lax.rem(me + k, group)}, device_id_type=pl.DeviceIdType.MESH
+        )
+    pl.semaphore_wait(barrier, group - 1)
+    for k in others:
+        copy(k).start()
+    keep = pltpu.make_async_copy(own, all_ref.at[me], keep_sem)
+    keep.start()
+    keep.wait()
+    for k in others:
+        copy(k).wait()
+
+
+def share(own, group):
+    hbm = pl.BlockSpec(memory_space=pl.ANY)
+    dma = pltpu.SemaphoreType.DMA
+    return pl.pallas_call(
+        functools.partial(share_kernel, group=group),
+        in_specs=[hbm],
+        out_specs=hbm,
+        out_shape=jax.ShapeDtypeStruct((group, *own.shape), own.dtype),
+        scratch_shapes=[dma((group,)), dma((group,)), dma],
+        compiler_params=pltpu.CompilerParams(collective_id=1, has_side_effects=True),
+        name="share",
+    )(own)
+
+
+def grad_x_kernel(*refs, first, inv_tokens, resume):
     if resume:
         z_ref, w_ref, top_ref, inv_ref, lab_ref, g_in, g_ref, dx_ref, hit_ref, g_even, g_odd, hits, sem = refs
     else:
@@ -305,10 +345,10 @@
     rows, cols = z_ref.shape
     chunks = g_even.shape[1] // cols
 
-    def make_g(dst):
+    def make_g(dst, low=0, high=None):
         begin = jnp.minimum(step, chunks - 1) * cols
         lane = lax.broadcasted_iota(jnp.int32, (1, LANES), 1) + begin
-        for r in range(0, rows, PART):
+        for r in range(low, rows if high is None else high, PART):
             here = slice(r, r + PART)
             top, inv, lab, found = top_ref[here, :], inv_ref[here, :], lab_ref[here, :], hits[here, :]
             for c in range(0, cols, LANES):
@@ -321,12 +361,17 @@
                     dst[here, pl.ds(pl.multiple_of(begin + c, LANES), LANES)] = g
             hits[here, :] = found
 
-    def product(src):
-        for r in range(0, rows, X_SUB):
+    def product(src, low=0, high=None):
+        for r in range(low, rows if high is None else high, X_SUB):
             dx_ref[r : r + X_SUB, :] = lax.dot_general(
                 src[r : r + X_SUB, :], w_ref[...], (((1,), (1,)), ((), ())), preferred_element_type=F32
             )
 
+    def both(src, dst):
+        for r in range(0, rows, MIX):
+            product(src, r, r + MIX)
+            make_g(dst, r, r + MIX)
+
     @pl.when(step == 0)
     def _():
         hits[...] = jnp.zeros_like(hits)
@@ -340,8 +385,7 @@
 
         @pl.when(block == 0)
         def _():
-            product(g_even)
-            make_g(g_odd)
+            both(g_even, g_odd)
 
         @pl.when(block == 1)
         def _():
@@ -353,13 +397,11 @@
 
         @pl.when(block == 1)
         def _():
-            product(g_even)
-            make_g(g_odd)
+            both(g_even, g_odd)
 
         @pl.when(block == 2)
         def _():
-            product(g_odd)
-            make_g(None)
+            both(g_odd, None)
 
     @pl.when(step == steps - 1)
     def _():
@@ -389,7 +431,7 @@
     stat = pl.BlockSpec((G_ROWS, LANES), lambda i, h: (row(i), 0))
     scratch = [pltpu.VMEM((G_ROWS, vocab), BF16)] * 2 + [pltpu.VMEM((G_ROWS, LANES), F32)]
     return pl.pallas_call(
-        functools.partial(grad_x_kernel, first=blocks, blocks=blocks, inv_tokens=inv_tokens, resume=resume),
+        functools.partial(grad_x_kernel, first=blocks, inv_tokens=inv_tokens, resume=resume),
         grid=grid,
         in_specs=[pl.BlockSpec((G_ROWS, G_COLS), chunk), pl.BlockSpec((X_TILE, vocab), w_block), stat, stat, stat]
         + ([pl.BlockSpec(memory_space=pl.ANY)] if resume else []),
@@ -424,11 +466,13 @@
         spread = lambda a: jnp.broadcast_to(a.reshape(-1, 1), (2 * tokens, LANES))
         top, inv, lab = spread(row_max), spread(1.0 / (row_sum * tokens)), spread(labels)
         g, part_a, hit_a = grad_x_call(z, w, top, inv, lab, 1.0 / tokens)
-        grad_x_a = lax.psum_scatter(part_a, "tp", scatter_dimension=0, tiled=True).astype(BF16)
+        sum_a = lax.psum_scatter(part_a, "tp", scatter_dimension=0, tiled=True)
         g, part_b, hit_b = grad_x_call(z, w, top, inv, lab, 1.0 / tokens, g)
-        grad_x_b = lax.psum_scatter(part_b, "tp", scatter_dimension=0, tiled=True).astype(BF16)
+        sum_b = lax.psum_scatter(part_b, "tp", scatter_dimension=0, tiled=True)
+        grad_x_a, grad_x_b = sum_a.astype(BF16), sum_b.astype(BF16)
         own = jnp.stack([jnp.sum(hit_a[:16]), jnp.sum(hit_a[16:]) + jnp.sum(hit_b[:8])])
-        target = lax.psum(own, "tp")
+        shared = share(jnp.broadcast_to(own[:, None, None], (2, 8, LANES)), group)
+        target = jnp.sum(shared[:, :, 0, 0], axis=0)
         losses = jnp.mean(row_max + jnp.log(row_sum), axis=-1) - target / tokens
         pair = lambda a: a.reshape(2, tokens, -1)
         grad_w = jnp.einsum("mth,mtv->hv", pair(x_full), pair(g), preferred_element_type=F32).astype(BF16)

time: 1000 us -> 997 us (level)
  blocking collectives: 14.4 us -> 0 us
    psum x1 -> x0, blocking collectives: 14.4 us -> none  [local_step(): target = lax.psum(own, 'tp')]
    pallas_call x2 -> x3, Pallas kernels: 306 us -> 309 us  [the longest x2 302 us: grad_x_call(): pl.pallas_call(functools.partial(grad_x_kernel, first=blocks, inv_tokens=...]
  transfers between devices with their start and end apart: 2 -> 2, of which waited for: 1 -> 1; matrix products, arithmetic and copies ran while one was open for 26% -> 26% of each run, Pallas kernels for 0% -> 1%
where the time goes in v2:
time: 997 us; the launch traced here: 991 us
  Pallas kernels  591 us (59%)
  matrix products  249 us (25%)
  waiting for transfers between devices  111 us (11%)
  between operations  15.7 us (2%)
  other arithmetic  14.9 us (1%)
    pallas_call x2, Pallas kernels, grad_x_call(): pl.pallas_call(functools.partial(grad_x_kernel, first=blocks, inv_tokens=...  302 us
    pallas_call x1, Pallas kernels, gather_logits(): pl.pallas_call(functools.partial(logits_kernel, group=group, sub=sub), gr...  283 us
    dot_general x1, matrix products, local_step(): jnp.einsum('mth,mtv->hv', pair(x_full), pair(g), preferred_element_type=F32)  249 us
    reduce_scatter x1, waiting for transfers between devices, local_step(): sum_a = lax.psum_scatter(part_a, 'tp', scatter_dimension=0, tiled=True)  110 us
  transfers between devices with their start and end apart: 2, of which 1 were waited for; matrix products, arithmetic and copies ran while one was open for 26% of the time, Pallas kernels for 1%

profile of v2, /device:TPU:112, one launch (start us, length us, event | category | flops | bytes accessed | tf_op | source)
XLA Modules:
  0.0 991.4 jit_solution(1490125935156595540)
XLA Ops:
  7.3 1.3 pad_add_fusion.lab
  8.5 282.5 %gather_logits.1 = (f32[4096,6144]{1,0:T(8,128)}, bf16[4096,4608]{1,0:T(8,128)(2,1)}, s32[8,2,256]{2,1,0:T(2,128)}, f32[8,2,2,2048]{3,2,1,0:T(2,128)}) custom-call(bf16[256,4608]{1,0:T(8,128)(2,1)} %x_a.1, bf16[256,4608]{1,0:T(8,128)(2,1)} %x_b.1, s32[2,256]{1,0:T(2,128)} %pad_add_fusion.lab, bf16[4608,6144]{1,0:T(8,128)(2,1)} %refs_1_.3), custom_call_target="tpu_custom_call" | custom-call | flops 231928233984 | bytes 100663296 | tf_op jit(solution)/shard_map/gather_logits/pallas_call | solution.py:269
  291.0 1.1 slice.20
  292.1 1.2 copy.11
  293.3 0.7 subtract_bitcast_fusion
  294.2 0.6 add_reduce_fusion
  294.9 1.9 broadcast_in_dim.11.refs_2_
  296.8 1.9 broadcast_in_dim.12.refs_3_
  298.7 2.9 broadcast_in_dim.13.refs_4_
  301.6 161.0 %grad_x_a.1 = (bf16[4096,6144]{1,0:T(8,128)(2,1)}, f32[2048,4608]{1,0:T(8,128)}, f32[24,128]{1,0:T(8,128)}) custom-call(f32[4096,6144]{1,0:T(8,128)} %get-tuple-element.15.refs_0_, bf16[4608,6144]{1,0:T(8,128)(2,1)} %refs_1_.3, f32[4096,128]{1,0:T(8,128)} %broadcast_in_dim.11.refs_2_, f32[4096,128]{1,0:T(8,128)} %broadcast_in_dim.12.refs_3_, ...), custom_call_target="tpu_custom_call" | custom-call | flops 115964116992 | bytes 75497472 | tf_op jit(solution)/shard_map/grad_x_a/pallas_call | solution.py:433
  462.7 141.4 %grad_x_b.1 = (bf16[4096,6144]{1,0:T(8,128)(2,1)}, f32[2048,4608]{1,0:T(8,128)}, f32[16,128]{1,0:T(8,128)}) custom-call(f32[4096,6144]{1,0:T(8,128)} %get-tuple-element.15.refs_0_, bf16[4608,6144]{1,0:T(8,128)(2,1)} %refs_1_.3, f32[4096,128]{1,0:T(8,128)} %broadcast_in_dim.11.refs_2_, ...), custom_call_target="tpu_custom_call", output_to_operand_aliasing={{0}: (5, {})} | custom-call | flops 115964116992 | bytes 75497472 | tf_op jit(solution)/shard_map/grad_x_b/pallas_call | solution.py:433
  604.2 0.7 reduce-scatter.3.cloned.1.call-update
  605.0 0.6 slice_reduce_fusion.4
  605.6 0.6 slice_reduce_fusion.3
  607.5 0.6 slice_reduce_fusion.2
  608.1 0.7 pad_maximum_fusion
  608.8 0.7 broadcast_in_dim.28.own
  609.5 6.1 share.1
  615.6 0.9 slice_reduce_fusion.1
  616.6 0.5 multiply_subtract_fusion
  617.1 248.8 %convolution_convert_fusion = bf16[4608,6144]{1,0:T(8,128)(2,1)} fusion(bf16[4096,4608]{1,0:T(8,128)(2,1)} %get-tuple-element.20, bf16[4096,6144]{1,0:T(8,128)(2,1)} %get-tuple-element.21), kind=kOutput, calls=%fused_computation | convolution fusion | flops 231956545536 | bytes 144703488 | tf_op jit(solution)/shard_map/mth,mtv->hv/dot_general | solution.py:478
  865.8 4.1 convert_element_type.11
  869.9 110.4 %reduce-scatter.3.cloned.1.call-done = f32[256,4608]{1,0:T(8,128)} async-done(((f32[2048,4608]{1,0:T(8,128)}), f32[256,4608]{1,0:T(8,128)}) %reduce-scatter.3.cloned.1.call-update) | async-done | bytes 4718608 | tf_op jit(solution)/shard_map/reduce_scatter | solution.py:469
  980.3 4.0 convert_element_type.10
  (16 shorter events, 0.4 us)
Async XLA Ops:
  7.2 858.7 %reduce-scatter.5.cloned.1.call-start = ((), (), s32[]{:S(2)}) async-start(), calls=%async_computation.3 | async-start | bytes 42467328 | tf_op jit(solution)/shard_map/reduce_scatter | solution.py:471
  604.1 0.9 copy-start
  604.1 1.5 copy-start.1
  604.1 12.5 %copy-start.2 = (f32[2]{0:T(128)S(1)}, f32[2]{0:T(128)}, u32[]{:S(2)}) copy-start(f32[2]{0:T(128)} %get-tuple-element.24) | copy-start | bytes 28
  604.2 376.2 %reduce-scatter.3.cloned.1.call-start = ((), (), s32[]{:S(2)}) async-start(), calls=%async_computation.2 | async-start | bytes 42467328 | tf_op jit(solution)/shard_map/reduce_scatter | solution.py:469
Sparse Core Ops, SparseCore 0:
  604.3 187.9 reduce-scatter.4
  794.6 185.6 reduce-scatter.2
